TPU v7x, 32 devices: a whole 2x2x4 slice. The times are simulated.
32 devices in a mesh: pipe: 2 (over y), dp: 4 (over z), tensor: 4 (over x, core).
Axes of the slice: x: 2, y: 2, z: 4, core: 2. Of those that a mesh axis runs over, the one named last changes fastest.
Arguments:
- saved: bfloat16 [2, 2, 256, 1024], P('pipe', None, 'dp'), may hold values from -6 to 6
- top_grad: bfloat16 [2, 256, 1024], P(None, 'dp'), may hold values from -6 to 6
- gain: bfloat16 [2, 1024], P('pipe', 'dp'), may hold values from 0.25 to 1.75
- w_query: bfloat16 [2, 1024, 1536], P('pipe', 'dp', 'tensor'), may hold values from -0.1875 to 0.1875
- w_latent: bfloat16 [2, 1024, 576], P('pipe', 'dp'), may hold values from -0.1875 to 0.1875
- compressed_gain: bfloat16 [2, 512], P('pipe', 'dp'), may hold values from 0.25 to 1.75
- expand_weight: bfloat16 [2, 512, 2048], P('pipe', 'dp', 'tensor'), may hold values from -0.25 to 0.25
- w_output: bfloat16 [2, 1024, 1024], P('pipe', 'tensor', 'dp'), may hold values from -0.1875 to 0.1875
Outputs:
- input_grad: bfloat16 [2, 2, 256, 1024], P('pipe', None, ('dp', 'tensor'))
- grad_gain: float32 [2, 1024], P('pipe', 'dp')
- grad_query: float32 [2, 1024, 1536], P('pipe', 'dp', 'tensor')
- grad_latent: float32 [2, 1024, 576], P('pipe', 'dp')
- grad_latent_gain: float32 [2, 512], P('pipe', 'dp')
- grad_expand: float32 [2, 512, 2048], P('pipe', 'dp', 'tensor')
- grad_output: float32 [2, 1024, 1024], P('pipe', 'tensor', 'dp')
All inputs are finite; a program needn't handle non-finite values.
Results may differ from a plain program's by a relative error of at most 0.04.
Values may be sent and summed in bfloat16 or wider, within the bound.
A program may use at most 64 MiB of HBM per device.

v0:
```python
import jax
import jax.numpy as jnp
from jax import lax
from jax.sharding import PartitionSpec as P

NOPE = 128
ROPE = 64
VDIM = 128
COMPRESSED_RANK = 512
EPS = 1e-06


def passed_along(value, axis, steps):
    count = lax.axis_size(axis)
    first, last = (max(0, -steps), min(count, count - steps))
    return lax.ppermute(value, axis, [(source, source + steps) for source in range(first, last)])


def root_mean_scale(values, scale):
    return values * lax.rsqrt(jnp.mean(values * values, axis=-1, keepdims=True) + EPS) * scale


def rotary_angles(values):
    length = values.shape[0]
    half = values.shape[-1] // 2
    freq = jnp.exp(-jnp.log(10000.0) * jnp.arange(half, dtype=jnp.float32) / half)
    angle = jnp.arange(length, dtype=jnp.float32)[:, None] * freq[None, :]
    cosine = jnp.cos(angle)[:, None, :]
    sine = jnp.sin(angle)[:, None, :]
    first = values[..., :half]
    second = values[..., half:]
    return jnp.concatenate(
        [first * cosine - second * sine, second * cosine + first * sine], axis=-1
    )


def branch(normed, w_q, w_lat, latent_norm_gain, w_exp, w_out):
    length = normed.shape[0]
    heads = w_q.shape[1] // (NOPE + ROPE)
    rounded = normed.astype(jnp.bfloat16)
    query = jnp.dot(rounded, w_q, preferred_element_type=jnp.float32).reshape(
        length, heads, NOPE + ROPE
    )
    latent_state = jnp.dot(rounded, w_lat, preferred_element_type=jnp.float32)
    compressed_state = root_mean_scale(latent_state[:, :COMPRESSED_RANK], latent_norm_gain).astype(
        jnp.bfloat16
    )
    rotary_key_part = rotary_angles(latent_state[:, None, COMPRESSED_RANK:])[:, 0, :]
    expanded = jnp.dot(compressed_state, w_exp, preferred_element_type=jnp.float32).reshape(
        length, heads, NOPE + VDIM
    )
    key_nope = expanded[:, :, :NOPE]
    values = expanded[:, :, NOPE:].astype(jnp.bfloat16)
    query_rope = rotary_angles(query[:, :, NOPE:])
    scores = jnp.einsum("qhd,khd->hqk", query[:, :, :NOPE], key_nope) + jnp.einsum(
        "qhd,kd->hqk", query_rope, rotary_key_part
    )
    scores = scores * (NOPE + ROPE) ** (-0.5)
    causal = jnp.arange(length)[:, None] >= jnp.arange(length)[None, :]
    scores = jnp.where(causal[None], scores, -1e30)
    weights = jax.nn.softmax(scores, axis=-1).astype(jnp.bfloat16)
    mixed = jnp.einsum("hqk,khd->qhd", weights.astype(jnp.float32), values.astype(jnp.float32))
    mixed = mixed.astype(jnp.bfloat16).reshape(length, heads * VDIM)
    return jnp.dot(mixed, w_out, preferred_element_type=jnp.float32)


def shards(saved, top_grad, gain, w_query, w_latent, compressed_gain, expand_weight, w_output):
    gathered = (
        lax.all_gather(gain, "dp", axis=1, tiled=True),
        lax.all_gather(w_query, "dp", axis=1, tiled=True),
        lax.all_gather(w_latent, "dp", axis=1, tiled=True),
        lax.all_gather(compressed_gain, "dp", axis=1, tiled=True),
        lax.all_gather(expand_weight, "dp", axis=1, tiled=True),
        lax.all_gather(w_output, "dp", axis=2, tiled=True),
    )
    gain32 = gathered[0][0].astype(jnp.float32)
    query_all = gathered[1][0]
    latent_all = gathered[2][0]
    lgain32 = gathered[3][0].astype(jnp.float32)
    expand_all = gathered[4][0]
    output_all = gathered[5][0]
    sections = lax.axis_size("pipe")
    section_index = lax.axis_index("pipe")
    tensor_count = lax.axis_size("tensor")
    tensor_rank = lax.axis_index("tensor")
    micro_count = saved.shape[1]
    length = saved.shape[2]
    width = saved.shape[3]
    share = length // tensor_count

    def compute(normed, upstream):
        unused, pull = jax.vjp(
            lambda value: branch(value, query_all, latent_all, lgain32, expand_all, output_all),
            normed,
        )
        return pull(upstream.astype(jnp.float32))[0]

    def skip(normed, upstream):
        return jnp.zeros_like(normed)

    gain_total = jnp.zeros((width,), jnp.float32)
    results = jnp.zeros((micro_count, share, width), jnp.bfloat16)
    stored = jnp.zeros((micro_count, length, width), jnp.bfloat16)
    received = jnp.zeros((length, width), jnp.bfloat16)
    for tick in range(sections + micro_count - 1):
        micro = tick - (sections - 1 - section_index)
        active = jnp.logical_and(micro >= 0, micro < micro_count)
        picked = jnp.clip(micro, 0, micro_count - 1)
        x_rows = lax.dynamic_index_in_dim(saved[0], picked, 0, keepdims=False)
        top_rows = lax.dynamic_index_in_dim(top_grad, picked, 0, keepdims=False)
        arrived = received
        upstream = jnp.where(section_index == sections - 1, top_rows, arrived)
        x_float = x_rows.astype(jnp.float32)
        normed, norm_pull = jax.vjp(root_mean_scale, x_float, gain32)
        branch_grad = lax.cond(active, compute, skip, normed, upstream)
        d_normed = lax.psum(branch_grad.astype(jnp.bfloat16), "tensor").astype(jnp.float32)
        dx_norm, d_gain = norm_pull(d_normed)
        dx = (upstream.astype(jnp.float32) + dx_norm).astype(jnp.bfloat16)
        gain_total = gain_total + jnp.where(active, d_gain, 0.0)
        mine = lax.dynamic_slice_in_dim(dx, tensor_rank * share, share, 0)
        chosen = (jnp.arange(micro_count) == micro)[:, None, None]
        results = jnp.where(chosen, mine[None], results)
        stored = jnp.where(chosen, upstream[None], stored)
        received = passed_along(dx, "pipe", -1)
    totals = (
        jnp.zeros(query_all.shape, jnp.float32),
        jnp.zeros(latent_all.shape, jnp.float32),
        jnp.zeros(lgain32.shape, jnp.float32),
        jnp.zeros(expand_all.shape, jnp.float32),
        jnp.zeros(output_all.shape, jnp.float32),
    )
    for micro_index in range(micro_count):
        normed_again = root_mean_scale(saved[0, micro_index].astype(jnp.float32), gain32)
        unused, weight_pull = jax.vjp(
            lambda w_q, w_lat, lat_gain, w_exp, w_out: branch(
                normed_again, w_q, w_lat, lat_gain, w_exp, w_out
            ),
            query_all,
            latent_all,
            lgain32,
            expand_all,
            output_all,
        )
        cotangents = weight_pull(stored[micro_index].astype(jnp.float32))
        totals = tuple(
            (total + piece.astype(jnp.float32) for total, piece in zip(totals, cotangents))
        )
    gain_part = jnp.where(tensor_rank == 0, gain_total, 0.0)
    grad_q, grad_lat, grad_lg, grad_e, grad_o = totals
    out_q, part_lat, part_lg, out_e, out_o, part_gain = (
        lax.psum_scatter(grad_q.astype(jnp.bfloat16), "dp", scatter_dimension=0, tiled=True).astype(
            jnp.float32
        ),
        lax.psum_scatter(
            grad_lat.astype(jnp.bfloat16), "dp", scatter_dimension=0, tiled=True
        ).astype(jnp.float32),
        lax.psum_scatter(
            grad_lg.astype(jnp.bfloat16), "dp", scatter_dimension=0, tiled=True
        ).astype(jnp.float32),
        lax.psum_scatter(grad_e.astype(jnp.bfloat16), "dp", scatter_dimension=0, tiled=True).astype(
            jnp.float32
        ),
        lax.psum_scatter(grad_o.astype(jnp.bfloat16), "dp", scatter_dimension=1, tiled=True).astype(
            jnp.float32
        ),
        lax.psum_scatter(
            gain_part.astype(jnp.bfloat16), "dp", scatter_dimension=0, tiled=True
        ).astype(jnp.float32),
    )
    out_lat, out_lg, out_gain = (
        lax.psum(part_lat.astype(jnp.bfloat16), "tensor").astype(jnp.float32),
        lax.psum(part_lg.astype(jnp.bfloat16), "tensor").astype(jnp.float32),
        lax.psum(part_gain.astype(jnp.bfloat16), "tensor").astype(jnp.float32),
    )
    return (
        results[None],
        out_gain[None],
        out_q[None],
        out_lat[None],
        out_lg[None],
        out_e[None],
        out_o[None],
    )


def solution(mesh):
    in_specs = (
        P("pipe", None, "dp", None),
        P(None, "dp", None),
        P("pipe", "dp"),
        P("pipe", "dp", "tensor"),
        P("pipe", "dp", None),
        P("pipe", "dp"),
        P("pipe", "dp", "tensor"),
        P("pipe", "tensor", "dp"),
    )
    out_specs = (
        P("pipe", None, ("dp", "tensor"), None),
        P("pipe", "dp"),
        P("pipe", "dp", "tensor"),
        P("pipe", "dp", None),
        P("pipe", "dp"),
        P("pipe", "dp", "tensor"),
        P("pipe", "tensor", "dp"),
    )
    return jax.shard_map(shards, mesh=mesh, in_specs=in_specs, out_specs=out_specs, check_vma=False)
```

profile of v0, /device:TPU:0, one launch (start us, length us, event | category | flops | bytes accessed | tf_op | source)
XLA Modules:
  0.0 381.7 jit_solution(9613141689715986463)
XLA Ops:
  7.2 1.9 copy.179
  9.3 12.9 %all_gather.19 = bf16[1,1024]{1,0:T(2,128)(2,1)S(1)} all-gather(bf16[1,256]{1,0:T(2,128)(2,1)} %param.16), channel_id=1, replica_groups=mesh['pipe'=2,'dp'=4,'tensor'=4] {'dp'}, dimensions={1}, use_global_device_ids=true | all-gather | bytes 2560 | tf_op jit(solution)/shard_map/all_gather | solution.py:69
  22.2 8.1 %all_gather.21 = bf16[1,512]{1,0:T(2,128)(2,1)S(1)} all-gather(bf16[1,128]{1,0:T(2,128)(2,1)} %param.19), channel_id=1, replica_groups=mesh['pipe'=2,'dp'=4,'tensor'=4] {'dp'}, dimensions={1}, use_global_device_ids=true | all-gather | bytes 1280 | tf_op jit(solution)/shard_map/all_gather | solution.py:72
  32.3 22.0 %all_gather.18 = bf16[1,256,1024]{2,1,0:T(8,128)(2,1)} all-gather(bf16[1,256,256]{2,1,0:T(8,128)(2,1)S(1)} %copy-done.55), channel_id=1, replica_groups=mesh['pipe'=2,'dp'=4,'tensor'=4] {'dp'}, dimensions={2}, use_global_device_ids=true | all-gather | bytes 655360 | tf_op jit(solution)/shard_map/all_gather | solution.py:74
  54.3 16.2 %all_gather.22 = bf16[1,512,512]{2,1,0:T(8,128)(2,1)S(1)} all-gather(bf16[1,128,512]{2,1,0:T(8,128)(2,1)S(1)} %copy-done.56), channel_id=1, replica_groups=mesh['pipe'=2,'dp'=4,'tensor'=4] {'dp'}, dimensions={1}, use_global_device_ids=true | all-gather | bytes 655360 | tf_op jit(solution)/shard_map/all_gather | solution.py:73
  71.3 17.4 %all_gather.23 = bf16[1,1024,384]{2,1,0:T(8,128)(2,1)} all-gather(bf16[1,256,384]{2,1,0:T(8,128)(2,1)S(1)} %copy-done.42), channel_id=1, replica_groups=mesh['pipe'=2,'dp'=4,'tensor'=4] {'dp'}, dimensions={1}, use_global_device_ids=true | all-gather | bytes 983040 | tf_op jit(solution)/shard_map/all_gather | solution.py:70
  89.5 40.7 %all-reduce.59.cloned.1.call-done = bf16[64,1024]{1,0:T(8,128)(2,1)} async-done(((bf16[64,1024]{1,0:T(8,128)(2,1)}), bf16[64,1024]{1,0:T(8,128)(2,1)}) %all-reduce.59.cloned.1.call-update) | async-done | bytes 131088 | tf_op jit(solution)/shard_map/psum | solution.py:116
  132.5 1.9 convert_multiply_fusion.16
  138.6 2.7 collective-permute-done
  142.3 28.0 %conditional.4 = (bf16[64,1024]{1,0:T(8,128)(2,1)}) conditional(s32[]{:T(128)} %convert_element_type.460, () %tuple.34, (bf16[64,1024]{1,0:T(8,128)(2,1)S(1)}, bf16[256,1024]{1,0:T(8,128)(2,1)}, f32[1024]{0:T(1024)S(1)}, f32[64,1024]{1,0:T(8,128)}, bf16[1024,576]{1,0:T(8,128)(2,1)S(1)}, /*index=5*/f32[512]{0:T(512)S(1)}, ...), branch_computations={%region_11.12_spmd, %region_12.0_spmd} | conditional | flops 367509920 | bytes 12992140 | solution.py:115
  142.3 2.0 fusion.75
  144.3 2.0 fusion.74
  155.8 1.8 fusion.56
  168.0 2.2 fusion.47
  170.8 30.4 %all-reduce.61.cloned.1.call-done = bf16[64,1024]{1,0:T(8,128)(2,1)} async-done(((bf16[64,1024]{1,0:T(8,128)(2,1)}), bf16[64,1024]{1,0:T(8,128)(2,1)}) %all-reduce.61.cloned.1.call-update) | async-done | bytes 131088 | tf_op jit(solution)/shard_map/psum | solution.py:116
  210.2 1.7 collective-permute-done.1
  236.1 9.3 %conditional.5 = (bf16[64,1024]{1,0:T(8,128)(2,1)S(1)}) conditional(s32[]{:T(128)} %convert_element_type.467, () %tuple.36, (bf16[64,1024]{1,0:T(8,128)(2,1)S(1)}, bf16[256,1024]{1,0:T(8,128)(2,1)}, f32[1024]{0:T(1024)S(1)}, f32[64,1024]{1,0:T(8,128)S(1)}, bf16[1024,576]{1,0:T(8,128)(2,1)S(1)}, /*index=5*/f32[512]{0:T(512)S(1)}, ...), branch_computations={%region_21.22_spmd, %region_22.28_spmd} | conditional | flops 367509920 | bytes 10745208 | solution.py:115
  247.8 15.5 %reduce-scatter.11.cloned.1.call-done = bf16[256,256]{1,0:T(8,128)(2,1)} async-done(((bf16[256,1024]{1,0:T(8,128)(2,1)}), bf16[256,256]{1,0:T(8,128)(2,1)}) %reduce-scatter.11.cloned.1.call-update) | async-done | bytes 131088 | tf_op jit(solution)/shard_map/reduce_scatter | solution.py:163
  264.9 28.1 %reduce-scatter.7.cloned.1.call-done = bf16[256,576]{0,1:T(8,128)(2,1)} async-done(((bf16[1024,576]{0,1:T(8,128)(2,1)}), bf16[256,576]{0,1:T(8,128)(2,1)}) %reduce-scatter.7.cloned.1.call-update) | async-done | bytes 294928 | tf_op jit(solution)/shard_map/reduce_scatter | solution.py:154
  293.1 24.0 %reduce-scatter.5.cloned.1.call-done = bf16[256,384]{1,0:T(8,128)(2,1)} async-done(((bf16[1024,384]{1,0:T(8,128)(2,1)}), bf16[256,384]{1,0:T(8,128)(2,1)}) %reduce-scatter.5.cloned.1.call-update) | async-done | bytes 196624 | tf_op jit(solution)/shard_map/reduce_scatter | solution.py:151
  318.9 33.2 %all-reduce.63.cloned.1.call-done = (bf16[64,1024]{1,0:T(8,128)(2,1)}, bf16[1,256,576]{1,2,0:T(8,128)(2,1)}) async-done(((bf16[64,1024]{1,0:T(8,128)(2,1)}, bf16[1,256,576]{1,2,0:T(8,128)(2,1)}), (bf16[64,1024]{1,0:T(8,128)(2,1)}, bf16[1,256,576]{1,2,0:T(8,128)(2,1)})) %all-reduce.63.cloned.1.call-update) | async-done | bytes 426000 | tf_op jit(solution)/shard_map/psum | solution.py:116
  353.4 11.7 %all-reduce.54 = (bf16[1024]{0:T(1024)(128)(2,1)S(1)}, bf16[512]{0:T(512)(128)(2,1)S(1)}) all-reduce(bf16[1024]{0:T(1024)(128)(2,1)S(1)} %select_convert_fusion, bf16[512]{0:T(512)(128)(2,1)S(1)} %add_convert_fusion.2), channel_id=2, replica_groups=mesh['pipe'=2,'dp'=4,'tensor'=4] {'dp'}, use_global_device_ids=true, to_apply=%region_33.34.clone | all-reduce | flops 1536 | bytes 6144
  365.2 5.9 %all-reduce.52 = (bf16[1,256]{1,0:T(2,128)(2,1)S(1)}, bf16[1,128]{1,0:T(2,128)(2,1)S(1)}) all-reduce(bf16[1,256]{1,0:T(2,128)(2,1)S(1)} %broadcast_in_dim.412, bf16[1,128]{1,0:T(2,128)(2,1)S(1)} %dynamic-slice_bitcast_fusion), channel_id=1, replica_groups=mesh['pipe'=2,'dp'=4,'tensor'=4] {'tensor'}, use_global_device_ids=true, to_apply=%region_34.35 | all-reduce | flops 384 | bytes 1536 | tf_op jit(solution)/shard_map/psum | solution.py:173
  371.6 1.8 broadcast_in_dim.440
  (459 shorter events, 80.0 us)
Async XLA Ops:
  7.2 64.1 %copy-start.2 = (bf16[1,2,64,1024]{3,2,1,0:T(8,128)(2,1)S(1)}, bf16[1,2,64,1024]{3,2,1,0:T(8,128)(2,1)}, u32[]{:S(2)}) copy-start(bf16[1,2,64,1024]{3,2,1,0:T(8,128)(2,1)} %param.14) | copy-start | bytes 786436
  7.2 81.5 %all-gather.2.cloned.1.call-start = ((), (), s32[]{:S(2)}) async-start(), calls=%async_computation.4 | async-start | bytes 1638400 | tf_op jit(solution)/shard_map/all_gather | solution.py:71
  9.2 62.2 %copy-start.42 = (bf16[1,256,384]{2,1,0:T(8,128)(2,1)S(1)}, bf16[1,256,384]{2,1,0:T(8,128)(2,1)}, u32[]{:S(2)}) copy-start(bf16[1,256,384]{2,1,0:T(8,128)(2,1)} %param.17) | copy-start | bytes 589828
  9.2 121.0 %all-reduce.59.cloned.1.call-start = ((), (), s32[]{:S(2)}) async-start(), calls=%async_computation.5 | async-start | bytes 262144 | tf_op jit(solution)/shard_map/psum | solution.py:116
  31.4 57.3 %copy-start.84 = (f32[32]{0:T(128)}, f32[32]{0:T(128)S(1)}, u32[]{:S(2)}) copy-start(f32[32]{0:T(128)S(1)} %multiply_exponential_fusion.3) | copy-start | bytes 388
  32.3 56.4 %copy-start.8 = (bf16[64,1024]{1,0:T(8,128)(2,1)}, bf16[64,1024]{1,0:T(8,128)(2,1)S(1)}, u32[]{:S(2)}) copy-start(bf16[64,1024]{1,0:T(8,128)(2,1)S(1)} %select_bitcast_fusion) | copy-start | bytes 393220
  89.5 111.8 %all-reduce.61.cloned.1.call-start = ((), (), s32[]{:S(2)}) async-start(), calls=%async_computation.6 | async-start | bytes 262144 | tf_op jit(solution)/shard_map/psum | solution.py:116
  134.3 7.0 %collective-permute-start = (bf16[64,1024]{1,0:T(8,128)(2,1)S(1)}, bf16[64,1024]{1,0:T(8,128)(2,1)}, u32[]{:S(2)}, u32[]{:S(2)}) collective-permute-start(bf16[64,1024]{1,0:T(8,128)(2,1)S(1)} %get-tuple-element.188), channel_id=1, source_target_pairs={{16,0},{17,1},{18,2},{19,3},{20,4},{21,5},{22,6},{23,7},{24,8},{25... | collective-permute-start | bytes 393224 | tf_op jit(solution)/shard_map/ppermute | solution.py:16
  170.3 75.9 %reduce-scatter.9.cloned.1.call-start = ((), (), s32[]{:S(2)}) async-start(), calls=%async_computation.9 | async-start | bytes 655360 | tf_op jit(solution)/shard_map/reduce_scatter | solution.py:160
  205.1 6.9 %collective-permute-start.1 = (bf16[64,1024]{1,0:T(8,128)(2,1)S(1)}, bf16[64,1024]{1,0:T(8,128)(2,1)S(1)}, u32[]{:S(2)}, u32[]{:S(2)}) collective-permute-start(bf16[64,1024]{1,0:T(8,128)(2,1)S(1)} %fusion.178), channel_id=1, source_target_pairs={{16,0},{17,1},{18,2},{19,3},{20,4},{21,5},{22,6},{23,7},{24,8},{25... | collective-permute-start | bytes 393224 | tf_op jit(solution)/shard_map/ppermute | solution.py:16
  219.5 43.8 %reduce-scatter.11.cloned.1.call-start = ((), (), s32[]{:S(2)}) async-start(), calls=%async_computation.10 | async-start | bytes 655360 | tf_op jit(solution)/shard_map/reduce_scatter | solution.py:163
  223.4 69.7 %reduce-scatter.7.cloned.1.call-start = ((), (), s32[]{:S(2)}) async-start(), calls=%async_computation.8 | async-start | bytes 1474560 | tf_op jit(solution)/shard_map/reduce_scatter | solution.py:154
  226.7 90.4 %reduce-scatter.5.cloned.1.call-start = ((), (), s32[]{:S(2)}) async-start(), calls=%async_computation.7 | async-start | bytes 983040 | tf_op jit(solution)/shard_map/reduce_scatter | solution.py:151
  230.6 121.5 %all-reduce.63.cloned.1.call-start = ((), (), s32[]{:S(2)}) async-start(), calls=%async_computation.11 | async-start | bytes 851968 | tf_op jit(solution)/shard_map/psum | solution.py:116
  245.4 106.7 %copy-start.97 = (f32[64]{0:T(128)S(1)}, f32[64]{0:T(128)}, u32[]{:S(2)}) copy-start(f32[64]{0:T(128)} %copy-done.95) | copy-start | bytes 772
  245.4 107.8 %copy-start.111 = (f32[64]{0:T(128)S(1)}, f32[64]{0:T(128)}, u32[]{:S(2)}) copy-start(f32[64]{0:T(128)} %copy-done.110) | copy-start | bytes 772
  245.4 107.9 %copy-start.64 = (f32[1024]{0:T(1024)S(1)}, f32[1024]{0:T(1024)}, u32[]{:S(2)}) copy-start(f32[1024]{0:T(1024)} %get-tuple-element.94) | copy-start | bytes 12292
  245.4 107.9 %copy-start.65 = (f32[1024]{0:T(1024)S(1)}, f32[1024]{0:T(1024)}, u32[]{:S(2)}) copy-start(f32[1024]{0:T(1024)} %get-tuple-element.96) | copy-start | bytes 12292
  264.9 109.0 %copy-start.112 = (f32[16]{0:T(128)S(1)}, f32[16]{0:T(128)}, u32[]{:S(2)}) copy-start(f32[16]{0:T(128)} %dynamic-slice.7) | copy-start | bytes 196
  293.1 81.0 %copy-start.57 = (bf16[16,1024]{1,0:T(8,128)(2,1)S(1)}, bf16[16,1024]{1,0:T(8,128)(2,1)}, u32[]{:S(2)}) copy-start(bf16[16,1024]{1,0:T(8,128)(2,1)} %constant_dynamic-slice_fusion) | copy-start | bytes 98308
  293.1 81.0 %copy-start.58 = (bf16[16,1024]{1,0:T(8,128)(2,1)S(1)}, bf16[16,1024]{1,0:T(8,128)(2,1)}, u32[]{:S(2)}) copy-start(bf16[16,1024]{1,0:T(8,128)(2,1)} %constant_dynamic-slice_fusion.1) | copy-start | bytes 98308
  293.1 81.0 %copy-start.92 = (pred[2]{0:T(512)(128)(4,1)S(1)}, pred[2]{0:T(512)(128)(4,1)}, u32[]{:S(2)}) copy-start(pred[2]{0:T(512)(128)(4,1)} %get-tuple-element.237) | copy-start | bytes 10
  293.1 81.0 %copy-start.94 = (pred[2]{0:T(512)(128)(4,1)S(1)}, pred[2]{0:T(512)(128)(4,1)}, u32[]{:S(2)}) copy-start(pred[2]{0:T(512)(128)(4,1)} %get-tuple-element.238) | copy-start | bytes 10
  293.1 81.0 %copy-start.105 = (pred[2]{0:T(512)(128)(4,1)S(1)}, pred[2]{0:T(512)(128)(4,1)}, u32[]{:S(2)}) copy-start(pred[2]{0:T(512)(128)(4,1)} %iota_compare_fusion.10) | copy-start | bytes 10
  (105 other events, 440.4 us)
Sparse Core Ops, SparseCore 0:
  10.1 43.6 all-gather.1
  89.6 40.6 all-reduce.58
  170.4 30.8 all-reduce.60
  219.7 21.2 reduce-scatter.8
  243.0 20.2 reduce-scatter.10
  265.5 27.5 reduce-scatter.6
  295.4 21.7 reduce-scatter.4
  319.6 32.4 all-reduce.62
where the time goes:
time: 383 us; the launch traced here: 382 us
  waiting for transfers between devices  177 us (46%)
  blocking collectives  94.1 us (25%)
  matrix products  39 us (10%)
  other arithmetic  28 us (7%)
  local copies, waits for them, and re-layouts  23.4 us (6%)
  between operations  16.9 us (4%)
    psum x3, waiting for transfers between devices, shards(): lax.psum(branch_grad.astype(jnp.bfloat16), 'tensor').astype(jnp.float32)  104 us
    reduce_scatter x1, waiting for transfers between devices, shards(): lax.psum_scatter(grad_lat.astype(jnp.bfloat16), 'dp', scatter_dimension=0...  28.1 us
    reduce_scatter x1, waiting for transfers between devices, shards(): lax.psum_scatter(grad_q.astype(jnp.bfloat16), 'dp', scatter_dimension=0,...  24 us
    all_gather x1, blocking collectives, shards(): lax.all_gather(w_output, 'dp', axis=2, tiled=True)  22 us
    all_gather x1, blocking collectives, shards(): lax.all_gather(w_query, 'dp', axis=1, tiled=True)  17.4 us
    all_gather x1, blocking collectives, shards(): lax.all_gather(expand_weight, 'dp', axis=1, tiled=True)  16.2 us
    reduce_scatter x1, waiting for transfers between devices, shards(): lax.psum_scatter(grad_o.astype(jnp.bfloat16), 'dp', scatter_dimension=1,...  15.5 us
    all_gather x1, blocking collectives, shards(): lax.all_gather(gain, 'dp', axis=1, tiled=True)  12.9 us
  transfers between devices with their start and end apart: 10, of which 8 were waited for; matrix products, arithmetic and copies ran while one was open for 10% of the time, Pallas kernels for 0%

commit v1 on v0

--- a/solution.py
+++ b/solution.py
@@ -113,7 +113,9 @@
         x_float = x_rows.astype(jnp.float32)
         normed, norm_pull = jax.vjp(root_mean_scale, x_float, gain32)
         branch_grad = lax.cond(active, compute, skip, normed, upstream)
-        d_normed = lax.psum(branch_grad.astype(jnp.bfloat16), "tensor").astype(jnp.float32)
+        d_normed = jnp.sum(
+            lax.all_gather(branch_grad.astype(jnp.bfloat16), "tensor"), axis=0
+        ).astype(jnp.float32)
         dx_norm, d_gain = norm_pull(d_normed)
         dx = (upstream.astype(jnp.float32) + dx_norm).astype(jnp.bfloat16)
         gain_total = gain_total + jnp.where(active, d_gain, 0.0)

time: 383 us -> 319 us (0.83)
  waiting for transfers between devices: 177 us -> 93.8 us
  blocking collectives: 94.1 us -> 114 us
    psum x3 -> x1, waiting for transfers between devices: 104 us -> 32.5 us  [shards(): lax.psum(part_lat.astype(jnp.bfloat16), 'tensor').astype(jnp.float32)]
    all_gather x0 -> x3, blocking collectives: none -> 22 us  [shards(): lax.all_gather(branch_grad.astype(jnp.bfloat16), 'tensor')]
    reduce_scatter x1, waiting for transfers between devices: 15.5 us -> 0.01 us  [shards(): lax.psum_scatter(grad_o.astype(jnp.bfloat16), 'dp', scatter_dimension=1,...]
    ppermute x2, waiting for transfers between devices: 4.45 us -> 15.3 us  [passed_along(): lax.ppermute(value, axis, [(source, source + steps) for source in range(f...]
    reduce_scatter x1, waiting for transfers between devices: 28.1 us -> 22 us  [shards(): lax.psum_scatter(grad_lat.astype(jnp.bfloat16), 'dp', scatter_dimension=0...]
  transfers between devices with their start and end apart: 10 -> 8, of which waited for: 8 -> 5; matrix products, arithmetic and copies ran while one was open for 10% -> 12% of each run, Pallas kernels for 0% -> 0%
where the time goes in v1:
time: 319 us; the launch traced here: 318 us
  blocking collectives  114 us (36%)
  waiting for transfers between devices  93.8 us (29%)
  matrix products  39.4 us (12%)
  other arithmetic  28.7 us (9%)
  local copies, waits for them, and re-layouts  21.6 us (7%)
  between operations  16.8 us (5%)
    psum x1, waiting for transfers between devices, shards(): lax.psum(part_lat.astype(jnp.bfloat16), 'tensor').astype(jnp.float32)  32.5 us
    reduce_scatter x1, waiting for transfers between devices, shards(): lax.psum_scatter(grad_q.astype(jnp.bfloat16), 'dp', scatter_dimension=0,...  23.9 us
    reduce_scatter x1, waiting for transfers between devices, shards(): lax.psum_scatter(grad_lat.astype(jnp.bfloat16), 'dp', scatter_dimension=0...  22 us
    all_gather x3, blocking collectives, shards(): lax.all_gather(branch_grad.astype(jnp.bfloat16), 'tensor')  22 us
    all_gather x1, blocking collectives, shards(): lax.all_gather(w_output, 'dp', axis=2, tiled=True)  21.2 us
    all_gather x1, blocking collectives, shards(): lax.all_gather(w_query, 'dp', axis=1, tiled=True)  17.5 us
    all_gather x1, blocking collectives, shards(): lax.all_gather(expand_weight, 'dp', axis=1, tiled=True)  16.2 us
    ppermute x2, waiting for transfers between devices, passed_along(): lax.ppermute(value, axis, [(source, source + steps) for source in range(f...  15.3 us
  transfers between devices with their start and end apart: 8, of which 5 were waited for; matrix products, arithmetic and copies ran while one was open for 12% of the time, Pallas kernels for 0%

profile of v1, /device:TPU:0, one launch (start us, length us, event | category | flops | bytes accessed | tf_op | source)
XLA Modules:
  0.0 317.6 jit_solution(11545357821090042736)
XLA Ops:
  7.2 1.9 copy.179
  9.9 12.9 %all_gather.37 = bf16[1,1024]{1,0:T(2,128)(2,1)S(1)} all-gather(bf16[1,256]{1,0:T(2,128)(2,1)} %param.16), channel_id=1, replica_groups=mesh['pipe'=2,'dp'=4,'tensor'=4] {'dp'}, dimensions={1}, use_global_device_ids=true | all-gather | bytes 2560 | tf_op jit(solution)/shard_map/all_gather | solution.py:69
  22.8 8.1 %all_gather.39 = bf16[1,512]{1,0:T(2,128)(2,1)S(1)} all-gather(bf16[1,128]{1,0:T(2,128)(2,1)} %param.19), channel_id=1, replica_groups=mesh['pipe'=2,'dp'=4,'tensor'=4] {'dp'}, dimensions={1}, use_global_device_ids=true | all-gather | bytes 1280 | tf_op jit(solution)/shard_map/all_gather | solution.py:72
  34.2 21.2 %all_gather.36 = bf16[1,256,1024]{2,1,0:T(8,128)(2,1)} all-gather(bf16[1,256,256]{2,1,0:T(8,128)(2,1)S(1)} %copy-done.49), channel_id=1, replica_groups=mesh['pipe'=2,'dp'=4,'tensor'=4] {'dp'}, dimensions={2}, use_global_device_ids=true | all-gather | bytes 655360 | tf_op jit(solution)/shard_map/all_gather | solution.py:74
  55.4 16.2 %all_gather.40 = bf16[1,512,512]{2,1,0:T(8,128)(2,1)S(1)} all-gather(bf16[1,128,512]{2,1,0:T(8,128)(2,1)S(1)} %copy-done.50), channel_id=1, replica_groups=mesh['pipe'=2,'dp'=4,'tensor'=4] {'dp'}, dimensions={1}, use_global_device_ids=true | all-gather | bytes 655360 | tf_op jit(solution)/shard_map/all_gather | solution.py:73
  72.5 17.5 %all_gather.41 = bf16[1,1024,384]{2,1,0:T(8,128)(2,1)} all-gather(bf16[1,256,384]{2,1,0:T(8,128)(2,1)S(1)} %copy-done.36), channel_id=1, replica_groups=mesh['pipe'=2,'dp'=4,'tensor'=4] {'dp'}, dimensions={1}, use_global_device_ids=true | all-gather | bytes 983040 | tf_op jit(solution)/shard_map/all_gather | solution.py:70
  90.0 7.0 %all-gather = bf16[256,1024]{1,0:T(8,128)(2,1)S(1)} all-gather(bf16[64,1024]{1,0:T(8,128)(2,1)S(1)} %get-tuple-element.237), channel_id=2, replica_groups=mesh['pipe'=2,'dp'=4,'tensor'=4] {'tensor'}, dimensions={0}, use_global_device_ids=true | all-gather | bytes 655360 | tf_op jit(solution)/shard_map/all_gather | solution.py:117
  107.5 9.2 %collective-permute-done = bf16[64,1024]{1,0:T(8,128)(2,1)} collective-permute-done((bf16[64,1024]{1,0:T(8,128)(2,1)S(1)}, bf16[64,1024]{1,0:T(8,128)(2,1)}, u32[]{:S(2)}, u32[]{:S(2)}) %collective-permute-start) | collective-permute-done | bytes 131104 | tf_op jit(solution)/shard_map/ppermute | solution.py:16
  117.7 28.0 %conditional.4 = (bf16[64,1024]{1,0:T(8,128)(2,1)}) conditional(s32[]{:T(128)} %convert_element_type.466, () %tuple.34, (bf16[64,1024]{1,0:T(8,128)(2,1)S(1)}, bf16[256,1024]{1,0:T(8,128)(2,1)}, f32[1024]{0:T(1024)S(1)}, f32[64,1024]{1,0:T(8,128)}, bf16[1024,576]{1,0:T(8,128)(2,1)S(1)}, /*index=5*/f32[512]{0:T(512)S(1)}, ...), branch_computations={%region_11.12_spmd, %region_12.0_spmd} | conditional | flops 367509920 | bytes 12992140 | solution.py:115
  117.7 2.0 fusion.75
  119.7 2.0 fusion.74
  143.5 2.2 fusion.47
  145.6 8.0 %all-gather.1 = bf16[256,1024]{1,0:T(8,128)(2,1)} all-gather(bf16[64,1024]{1,0:T(8,128)(2,1)} %get-tuple-element.238), channel_id=3, replica_groups=mesh['pipe'=2,'dp'=4,'tensor'=4] {'tensor'}, dimensions={0}, use_global_device_ids=true | all-gather | bytes 655360 | tf_op jit(solution)/shard_map/all_gather | solution.py:117
  153.6 1.8 reduce_sum.377
  165.2 6.1 %collective-permute-done.1 = bf16[64,1024]{1,0:T(8,128)(2,1)S(1)} collective-permute-done((bf16[64,1024]{1,0:T(8,128)(2,1)S(1)}, bf16[64,1024]{1,0:T(8,128)(2,1)S(1)}, u32[]{:S(2)}, u32[]{:S(2)}) %collective-permute-start.1) | collective-permute-done | bytes 131104 | tf_op jit(solution)/shard_map/ppermute | solution.py:16
  179.3 1.8 multiply_reduce_fusion.11
  186.4 9.1 %conditional.5 = (bf16[64,1024]{1,0:T(8,128)(2,1)S(1)}) conditional(s32[]{:T(128)} %convert_element_type.473, () %tuple.36, (bf16[64,1024]{1,0:T(8,128)(2,1)S(1)}, bf16[256,1024]{1,0:T(8,128)(2,1)}, f32[1024]{0:T(1024)S(1)}, f32[64,1024]{1,0:T(8,128)S(1)}, bf16[1024,576]{1,0:T(8,128)(2,1)S(1)}, /*index=5*/f32[512]{0:T(512)S(1)}, ...), branch_computations={%region_21.22_spmd, %region_22.28_spmd} | conditional | flops 367509920 | bytes 10742024 | solution.py:115
  195.6 7.0 %all-gather.2 = bf16[256,1024]{1,0:T(8,128)(2,1)S(1)} all-gather(bf16[64,1024]{1,0:T(8,128)(2,1)S(1)} %get-tuple-element.239), channel_id=4, replica_groups=mesh['pipe'=2,'dp'=4,'tensor'=4] {'tensor'}, dimensions={0}, use_global_device_ids=true | all-gather | bytes 655360 | tf_op jit(solution)/shard_map/all_gather | solution.py:117
  206.7 10.2 %all-reduce.53 = (bf16[1024]{0:T(1024)(128)(2,1)S(1)}, bf16[512]{0:T(512)(128)(2,1)S(1)}) all-reduce(bf16[1024]{0:T(1024)(128)(2,1)S(1)} %select_convert_fusion, bf16[512]{0:T(512)(128)(2,1)S(1)} %add_convert_fusion.2), channel_id=5, replica_groups=mesh['pipe'=2,'dp'=4,'tensor'=4] {'dp'}, use_global_device_ids=true, to_apply=%region_33.34.clone | all-reduce | flops 1536 | bytes 6144
  217.1 5.6 %all-reduce.52 = (bf16[1,256]{1,0:T(2,128)(2,1)S(1)}, bf16[1,128]{1,0:T(2,128)(2,1)S(1)}) all-reduce(bf16[1,256]{1,0:T(2,128)(2,1)S(1)} %broadcast_in_dim.412, bf16[1,128]{1,0:T(2,128)(2,1)S(1)} %dynamic-slice_bitcast_fusion), channel_id=1, replica_groups=mesh['pipe'=2,'dp'=4,'tensor'=4] {'tensor'}, use_global_device_ids=true, to_apply=%region_34.35 | all-reduce | flops 384 | bytes 1536 | tf_op jit(solution)/shard_map/psum | solution.py:175
  228.8 22.0 %reduce-scatter.7.cloned.1.call-done = bf16[256,576]{0,1:T(8,128)(2,1)} async-done(((bf16[1024,576]{0,1:T(8,128)(2,1)}), bf16[256,576]{0,1:T(8,128)(2,1)}) %reduce-scatter.7.cloned.1.call-update) | async-done | bytes 294928 | tf_op jit(solution)/shard_map/reduce_scatter | solution.py:156
  250.8 23.9 %reduce-scatter.5.cloned.1.call-done = bf16[256,384]{1,0:T(8,128)(2,1)} async-done(((bf16[1024,384]{1,0:T(8,128)(2,1)}), bf16[256,384]{1,0:T(8,128)(2,1)}) %reduce-scatter.5.cloned.1.call-update) | async-done | bytes 196624 | tf_op jit(solution)/shard_map/reduce_scatter | solution.py:153
  276.4 32.5 %all-reduce.56.cloned.1.call-done = bf16[1,256,576]{1,2,0:T(8,128)(2,1)} async-done(((bf16[1,256,576]{1,2,0:T(8,128)(2,1)}), bf16[1,256,576]{1,2,0:T(8,128)(2,1)}) %all-reduce.56.cloned.1.call-update) | async-done | bytes 294928 | tf_op jit(solution)/shard_map/psum | solution.py:173
  308.9 1.8 broadcast_in_dim.440
  (443 shorter events, 79.3 us)
Async XLA Ops:
  7.2 26.3 %copy-start.2 = (bf16[1,2,64,1024]{3,2,1,0:T(8,128)(2,1)S(1)}, bf16[1,2,64,1024]{3,2,1,0:T(8,128)(2,1)}, u32[]{:S(2)}) copy-start(bf16[1,2,64,1024]{3,2,1,0:T(8,128)(2,1)} %param.14) | copy-start | bytes 786436
  7.2 27.1 %copy-start.49 = (bf16[1,256,256]{2,1,0:T(8,128)(2,1)S(1)}, bf16[1,256,256]{2,1,0:T(8,128)(2,1)}, u32[]{:S(2)}) copy-start(bf16[1,256,256]{2,1,0:T(8,128)(2,1)} %param.21) | copy-start | bytes 393220
  7.2 48.2 %copy-start.50 = (bf16[1,128,512]{2,1,0:T(8,128)(2,1)S(1)}, bf16[1,128,512]{2,1,0:T(8,128)(2,1)}, u32[]{:S(2)}) copy-start(bf16[1,128,512]{2,1,0:T(8,128)(2,1)} %param.20) | copy-start | bytes 393220
  7.2 82.7 %all-gather.5.cloned.1.call-start = ((), (), s32[]{:S(2)}) async-start(), calls=%async_computation.4 | async-start | bytes 1638400 | tf_op jit(solution)/shard_map/all_gather | solution.py:71
  9.2 216.3 %reduce-scatter.9.cloned.1.call-start = ((), (), s32[]{:S(2)}) async-start(), calls=%async_computation.8 | async-start | bytes 655360 | tf_op jit(solution)/shard_map/reduce_scatter | solution.py:162
  9.3 63.2 %copy-start.36 = (bf16[1,256,384]{2,1,0:T(8,128)(2,1)S(1)}, bf16[1,256,384]{2,1,0:T(8,128)(2,1)}, u32[]{:S(2)}) copy-start(bf16[1,256,384]{2,1,0:T(8,128)(2,1)} %param.17) | copy-start | bytes 589828
  9.9 80.1 %copy-start.82 = (f32[32]{0:T(128)}, f32[32]{0:T(128)S(1)}, u32[]{:S(2)}) copy-start(f32[32]{0:T(128)S(1)} %multiply_exponential_fusion.3) | copy-start | bytes 388
  33.5 56.4 %copy-start.9 = (bf16[64,1024]{1,0:T(8,128)(2,1)}, bf16[64,1024]{1,0:T(8,128)(2,1)S(1)}, u32[]{:S(2)}) copy-start(bf16[64,1024]{1,0:T(8,128)(2,1)S(1)} %select_bitcast_fusion) | copy-start | bytes 393220
  99.5 17.2 %collective-permute-start = (bf16[64,1024]{1,0:T(8,128)(2,1)S(1)}, bf16[64,1024]{1,0:T(8,128)(2,1)}, u32[]{:S(2)}, u32[]{:S(2)}) collective-permute-start(bf16[64,1024]{1,0:T(8,128)(2,1)S(1)} %get-tuple-element.186), channel_id=1, source_target_pairs={{16,0},{17,1},{18,2},{19,3},{20,4},{21,5},{22,6},{23,7},{24,8},{25... | collective-permute-start | bytes 393224 | tf_op jit(solution)/shard_map/ppermute | solution.py:16
  101.3 16.3 %copy-start = (bf16[1,1024,576]{2,1,0:T(8,128)(2,1)S(1)}, bf16[1,1024,576]{2,1,0:T(8,128)(2,1)}, u32[]{:S(2)}) copy-start(bf16[1,1024,576]{2,1,0:T(8,128)(2,1)} %all-gather.5.cloned.1.call-done) | copy-start | bytes 3538948
  157.5 19.6 %copy-start.3 = (f32[64,576]{1,0:T(8,128)}, f32[64,576]{1,0:T(8,128)S(1)}, u32[]{:S(2)}) copy-start(f32[64,576]{1,0:T(8,128)S(1)} %fusion.196) | copy-start | bytes 442372
  159.1 18.1 %copy-start.77 = (f32[64]{0:T(128)}, f32[64]{0:T(128)S(1)}, u32[]{:S(2)}) copy-start(f32[64]{0:T(128)S(1)} %fusion.265) | copy-start | bytes 772
  159.1 16.2 %copy-start.78 = (f32[64]{0:T(128)}, f32[64]{0:T(128)S(1)}, u32[]{:S(2)}) copy-start(f32[64]{0:T(128)S(1)} %fusion.264) | copy-start | bytes 772
  162.2 9.1 %collective-permute-start.1 = (bf16[64,1024]{1,0:T(8,128)(2,1)S(1)}, bf16[64,1024]{1,0:T(8,128)(2,1)S(1)}, u32[]{:S(2)}, u32[]{:S(2)}) collective-permute-start(bf16[64,1024]{1,0:T(8,128)(2,1)S(1)} %fusion.178), channel_id=1, source_target_pairs={{16,0},{17,1},{18,2},{19,3},{20,4},{21,5},{22,6},{23,7},{24,8},{25... | collective-permute-start | bytes 393224 | tf_op jit(solution)/shard_map/ppermute | solution.py:16
  178.4 48.7 %reduce-scatter.11.cloned.1.call-start = ((), (), s32[]{:S(2)}) async-start(), calls=%async_computation.9 | async-start | bytes 655360 | tf_op jit(solution)/shard_map/reduce_scatter | solution.py:165
  183.2 67.6 %reduce-scatter.7.cloned.1.call-start = ((), (), s32[]{:S(2)}) async-start(), calls=%async_computation.6 | async-start | bytes 1474560 | tf_op jit(solution)/shard_map/reduce_scatter | solution.py:156
  186.3 88.4 %reduce-scatter.5.cloned.1.call-start = ((), (), s32[]{:S(2)}) async-start(), calls=%async_computation.5 | async-start | bytes 983040 | tf_op jit(solution)/shard_map/reduce_scatter | solution.py:153
  205.1 18.7 %copy-start.105 = (f32[16]{0:T(128)S(1)}, f32[16]{0:T(128)}, u32[]{:S(2)}) copy-start(f32[16]{0:T(128)} %dynamic-slice.7) | copy-start | bytes 196
  205.1 19.6 %copy-start.52 = (bf16[16,1024]{1,0:T(8,128)(2,1)S(1)}, bf16[16,1024]{1,0:T(8,128)(2,1)}, u32[]{:S(2)}) copy-start(bf16[16,1024]{1,0:T(8,128)(2,1)} %constant_dynamic-slice_fusion) | copy-start | bytes 98308
  205.1 19.6 %copy-start.53 = (bf16[16,1024]{1,0:T(8,128)(2,1)S(1)}, bf16[16,1024]{1,0:T(8,128)(2,1)}, u32[]{:S(2)}) copy-start(bf16[16,1024]{1,0:T(8,128)(2,1)} %constant_dynamic-slice_fusion.1) | copy-start | bytes 98308
  205.1 19.6 %copy-start.88 = (pred[2]{0:T(512)(128)(4,1)S(1)}, pred[2]{0:T(512)(128)(4,1)}, u32[]{:S(2)}) copy-start(pred[2]{0:T(512)(128)(4,1)} %get-tuple-element.235) | copy-start | bytes 10
  205.1 19.6 %copy-start.90 = (pred[2]{0:T(512)(128)(4,1)S(1)}, pred[2]{0:T(512)(128)(4,1)}, u32[]{:S(2)}) copy-start(pred[2]{0:T(512)(128)(4,1)} %get-tuple-element.236) | copy-start | bytes 10
  205.1 19.6 %copy-start.98 = (pred[2]{0:T(512)(128)(4,1)S(1)}, pred[2]{0:T(512)(128)(4,1)}, u32[]{:S(2)}) copy-start(pred[2]{0:T(512)(128)(4,1)} %iota_compare_fusion.10) | copy-start | bytes 10
  206.5 102.4 %all-reduce.56.cloned.1.call-start = ((), (), s32[]{:S(2)}) async-start(), calls=%async_computation.7 | async-start | bytes 589824 | tf_op jit(solution)/shard_map/psum | solution.py:173
  (95 other events, 362.6 us)
Sparse Core Ops, SparseCore 0:
  10.1 43.3 all-gather.4
  178.5 20.0 reduce-scatter.8
  200.9 20.1 reduce-scatter.10
  223.2 27.5 reduce-scatter.6
  252.9 21.7 reduce-scatter.4
  276.9 31.9 all-reduce.55
